TPU v7x, 32 devices: a whole 2x2x4 slice. The times are simulated.
32 devices in a mesh: tm: 8 (over z, y), tensor: 4 (over x, core).
Axes of the slice: x: 2, y: 2, z: 4, core: 2. Of those that a mesh axis runs over, the one named last changes fastest.
Arguments:
- frames_in: bfloat16 [8, 528, 1024], P('tm'), may hold values from -6 to 6
- frame_time: int32 [8], replicated, may hold values from 0 to 7, each once
- cond_count: int32 [8], replicated, may hold values from 0 to 2
- ln1_gain: float32 [2, 1024], replicated, may hold values from 0.5 to 1.5
- ln1_bias: float32 [2, 1024], replicated, may hold values from -1.75 to 1.75
- qkv_weight: bfloat16 [2, 3, 1024, 1024], P(None, None, None, 'tensor'), may hold values from -17 to 17
- qkv_bias: float32 [2, 3, 1024], P(None, None, 'tensor'), may hold values from -1.75 to 1.75
- out_weight: bfloat16 [2, 1024, 1024], P(None, 'tensor'), may hold values from -0.1875 to 0.1875
- out_bias: float32 [2, 1024], replicated, may hold values from -1.75 to 1.75
- ln2_gain: float32 [2, 1024], replicated, may hold values from 0.5 to 1.5
- ln2_bias: float32 [2, 1024], replicated, may hold values from -1.75 to 1.75
- fc1_weight: bfloat16 [2, 1024, 4096], P(None, None, 'tensor'), may hold values from -0.1875 to 0.1875
- fc1_bias: float32 [2, 4096], P(None, 'tensor'), may hold values from -3 to 3
- fc2_weight: bfloat16 [2, 4096, 1024], P(None, 'tensor'), may hold values from -0.09375 to 0.09375
- fc2_bias: float32 [2, 1024], replicated, may hold values from -1.75 to 1.75
Outputs:
- frames_out: bfloat16 [8, 528, 1024], P('tm', 'tensor')
Inputs may be any that keep to these rules, and one draw needn't show every extreme that they name: `frame_time`: every time index 0 to 7 appears once. `cond_count`: the valid action and state tokens of a frame are its first ones.
All inputs are finite; a program needn't handle non-finite values.
Results may differ from a plain program's by a relative error of at most 0.04.
Values may be sent and summed in bfloat16 or wider, within the bound.
A program may use at most 128 MiB of HBM per device.

v0:
```python
import jax
import jax.numpy as jnp
from jax import lax
from jax.sharding import PartitionSpec as P

D = 1024
HEADS = 16
PATCH_DEV = 64
COND = 2
LAYERS = 2


def layer_norm(inputs, gain_row, bias_row):
    center = jnp.mean(inputs, axis=-1, keepdims=True)
    spread = jnp.mean(jnp.square(inputs - center), axis=-1, keepdims=True)
    return (inputs - center) * lax.rsqrt(spread + 1e-06) * gain_row + bias_row


def piece_tables(frame_time, cond_count, piece_count, frame_split, piece_rows):
    cond_dev = COND // frame_split
    piece_ids = jnp.arange(piece_count, dtype=jnp.int32)
    frame_ids = jnp.arange(frame_time.shape[0], dtype=jnp.int32)
    matches = (piece_ids // frame_split)[:, None] == frame_ids[None, :]
    piece_time = jnp.sum(jnp.where(matches, frame_time[None, :], 0), axis=1)
    piece_cond = jnp.sum(jnp.where(matches, cond_count[None, :], 0), axis=1)
    slot_index = jnp.arange(piece_rows, dtype=jnp.int32)
    cond_slot = (piece_ids % frame_split)[:, None] * cond_dev + slot_index[None, :] - PATCH_DEV
    valid = (slot_index[None, :] < PATCH_DEV) | (cond_slot < piece_cond[:, None])
    return (piece_time, valid)


def shards(
    frames_in,
    frame_time,
    cond_count,
    ln1_gain,
    ln1_bias,
    qkv_weight,
    qkv_bias,
    out_weight,
    out_bias,
    ln2_gain,
    ln2_bias,
    fc1_weight,
    fc1_bias,
    fc2_weight,
    fc2_bias,
):
    frame_count = frame_time.shape[0]
    piece_count = lax.axis_size("tm")
    frame_split = piece_count // frame_count
    cond_dev = COND // frame_split
    piece_rows = PATCH_DEV + cond_dev
    row_count = frames_in.shape[1]
    seq_count = row_count // piece_rows
    head_dim = D // HEADS
    head_local = qkv_weight.shape[3] // head_dim
    scale = head_dim ** (-0.5)
    tensor_size = lax.axis_size("tensor")
    tensor_pos = lax.axis_index("tensor")
    my_piece = lax.axis_index("tm")
    share_rows = row_count // tensor_size
    piece_time, valid = piece_tables(frame_time, cond_count, piece_count, frame_split, piece_rows)
    piece_ids = jnp.arange(piece_count, dtype=jnp.int32)
    my_time = jnp.sum(jnp.where(piece_ids == my_piece, piece_time, 0))
    full_in = frames_in[0]
    new_share = None
    for layer_idx in range(LAYERS):
        normed = layer_norm(
            full_in.astype(jnp.float32), ln1_gain[layer_idx], ln1_bias[layer_idx]
        ).astype(jnp.bfloat16)
        projected = jnp.einsum(
            "rd,jde->jre", normed, qkv_weight[layer_idx], preferred_element_type=jnp.float32
        )
        projected = (projected + qkv_bias[layer_idx][:, None, :]).astype(jnp.bfloat16)
        queries = projected[0].reshape(seq_count, piece_rows, head_local, head_dim)
        keys_mine = projected[1].reshape(1, seq_count, piece_rows, head_local * head_dim)
        values_mine = projected[2].reshape(1, seq_count, piece_rows, head_local * head_dim)
        start_top = jnp.full((seq_count, head_local, piece_rows), -1e30, jnp.float32)
        key_block = lax.all_gather(keys_mine, "tm", axis=0, tiled=True)
        value_block = lax.all_gather(values_mine, "tm", axis=0, tiled=True)
        block_count = key_block.shape[0]
        block_ids = jnp.arange(block_count, dtype=jnp.int32)
        matches = block_ids[:, None] == piece_ids[None, :]
        key_time = jnp.sum(jnp.where(matches, piece_time[None, :], 0), axis=1)
        key_valid = jnp.any(matches[:, :, None] & valid[None, :, :], axis=1)
        allowed = (key_time <= my_time)[:, None] & key_valid
        top_run = start_top
        keys_split = key_block.reshape(block_count, seq_count, piece_rows, head_local, head_dim)
        values_split = value_block.reshape(block_count, seq_count, piece_rows, head_local, head_dim)
        scores = (
            jnp.einsum("sqhd,gskhd->shqgk", queries, keys_split, preferred_element_type=jnp.float32)
            * scale
        )
        scores = jnp.where(allowed, scores, -1e30)
        new_top = jnp.maximum(top_run, jnp.max(scores, axis=(3, 4)))
        weights = jnp.where(allowed, jnp.exp(scores - new_top[..., None, None]), 0.0)
        total_new = jnp.sum(weights, axis=(3, 4))
        mixed = jnp.einsum(
            "shqgk,gskhd->shqd",
            weights.astype(jnp.bfloat16),
            values_split,
            preferred_element_type=jnp.float32,
        )
        top_run = new_top
        attended = (
            (mixed / total_new[..., None])
            .transpose(0, 2, 1, 3)
            .reshape(row_count, head_local * head_dim)
            .astype(jnp.bfloat16)
        )
        out_layer = out_weight[layer_idx]
        fc1_layer = fc1_weight[layer_idx]
        fc2_layer = fc2_weight[layer_idx]
        fc1_layer_bias = fc1_bias[layer_idx]
        own_rows = lax.dynamic_slice_in_dim(full_in, tensor_pos * share_rows, share_rows, 0).astype(
            jnp.float32
        )
        first = (
            own_rows
            + lax.psum_scatter(
                jnp.dot(attended, out_layer, preferred_element_type=jnp.float32).astype(
                    jnp.bfloat16
                ),
                "tensor",
                scatter_dimension=0,
                tiled=True,
            ).astype(jnp.float32)
            + out_bias[layer_idx]
        )
        normed_two = layer_norm(first, ln2_gain[layer_idx], ln2_bias[layer_idx]).astype(
            jnp.bfloat16
        )
        inner = jax.nn.gelu(
            jnp.dot(
                lax.all_gather(normed_two, "tensor", axis=0, tiled=True),
                fc1_layer,
                preferred_element_type=jnp.float32,
            )
            + fc1_layer_bias,
            approximate=False,
        ).astype(jnp.bfloat16)
        mlp_share = lax.psum_scatter(
            jnp.dot(inner, fc2_layer, preferred_element_type=jnp.float32).astype(jnp.bfloat16),
            "tensor",
            scatter_dimension=0,
            tiled=True,
        ).astype(jnp.float32)
        new_share = (first + mlp_share + fc2_bias[layer_idx]).astype(jnp.bfloat16)
        if layer_idx + 1 < LAYERS:
            full_in = lax.all_gather(new_share, "tensor", axis=0, tiled=True)
    return new_share[None]


def solution(mesh):
    in_specs = (
        P("tm", None, None),
        P(),
        P(),
        P(),
        P(),
        P(None, None, None, "tensor"),
        P(None, None, "tensor"),
        P(None, "tensor", None),
        P(),
        P(),
        P(),
        P(None, None, "tensor"),
        P(None, "tensor"),
        P(None, "tensor", None),
        P(),
    )
    out_specs = P("tm", "tensor", None)
    return jax.shard_map(shards, mesh=mesh, in_specs=in_specs, out_specs=out_specs, check_vma=False)
```

profile of v0, /device:TPU:0, one launch (start us, length us, event | category | flops | bytes accessed | tf_op | source)
XLA Modules:
  0.0 451.9 jit_solution(13556818478899663890)
XLA Ops:
  6.6 1.6 convert_reduce_fusion
  8.1 1.7 fusion.32
  11.6 2.6 fusion.91
  19.8 48.0 %all-gather.11.cloned.1.call-done = bf16[8,8,66,256]{3,1,2,0:T(8,128)(2,1)} async-done(((bf16[1,8,66,256]{3,1,2,0:T(8,128)(2,1)}), bf16[8,8,66,256]{3,1,2,0:T(8,128)(2,1)}) %all-gather.11.cloned.1.call-update) | async-done | bytes 2162704 | tf_op jit(solution)/shard_map/all_gather | solution.py:80
  67.9 7.2 %reshape.170 = bf16[8,8,66,4,64]{4,3,1,2,0:T(4,128)(2,1)} reshape(bf16[8,8,66,256]{3,1,2,0:T(8,128)(2,1)} %all-gather.11.cloned.1.call-done) | data formatting | bytes 4325376 | tf_op jit(solution)/shard_map/reshape | solution.py:89
  75.1 8.7 %fusion.18 = f32[8,4,66,8,66]{2,4,3,1,0:T(8,128)} fusion(bf16[8,8,66,4,64]{4,3,1,2,0:T(4,128)(2,1)} %reshape.170, bf16[8,66,4,64,1]{3,2,1,0,4:T(4,128)(2,1)S(1)} %bitcast.144), kind=kOutput, calls=%fused_computation.18 | convolution fusion | flops 142737408 | bytes 6893568 | tf_op jit(solution)/shard_map/sqhd,gskhd->shqgk/dot_general | solution.py:92
  83.8 10.7 %copy.65 = f32[8,4,66,8,66]{4,3,2,1,0:T(8,128)} copy(f32[8,4,66,8,66]{2,4,3,1,0:T(8,128)} %fusion.18) | data formatting | bytes 8921088 | tf_op jit(solution)/shard_map/sqhd,gskhd->shqgk/dot_general | solution.py:92
  94.5 8.5 %fusion.4 = f32[8,4,66]{2,1,0:T(4,128)S(1)} fusion(f32[8,4,66,8,66]{4,3,2,1,0:T(8,128)} %copy.65, pred[8,66]{1,0:T(8,128)(4,1)S(1)} %broadcast_and_fusion), kind=kLoop, calls=%fused_computation.4 | loop fusion | flops 3343296 | bytes 4469520 | tf_op jit(solution)/shard_map/reduce_max | solution.py:96
  103.0 31.2 %fusion.6 = (f32[8,4,66]{2,1,0:T(4,128)S(1)}, bf16[8,4,66,8,66]{4,3,2,1,0:T(8,128)(2,1)}) fusion(f32[8,4,66,8,66]{4,3,2,1,0:T(8,128)S(1)} %copy-done.1, f32[8,4,66]{2,1,0:T(4,128)S(1)} %broadcast_maximum_fusion.1, pred[8,66]{1,0:T(8,128)(4,1)S(1)} %broadcast_and_fusion), kind=kLoop, calls=%fused_computation.6 | loop fusion | flops 6688704 | bytes 6708240 | tf_op jit(solution)/shard_map/reduce_sum | solution.py:98
  134.2 7.4 %reshape.171 = bf16[8,8,66,4,64]{4,3,1,2,0:T(4,128)(2,1)} reshape(bf16[8,8,66,256]{3,1,2,0:T(8,128)(2,1)} %all-gather.13.cloned.1.call-done) | data formatting | bytes 4325376 | tf_op jit(solution)/shard_map/reshape | solution.py:90
  141.6 8.5 %divide_convert_fusion.1 = bf16[8,66,4,64]{1,3,2,0:T(8,128)(2,1)S(1)} fusion(bf16[8,8,66,4,64]{4,3,1,2,0:T(4,128)(2,1)} %reshape.171, bf16[8,4,66,8,66]{4,3,2,1,0:T(8,128)(2,1)} %get-tuple-element.8, f32[8,66,4]{1,2,0:T(4,128)S(1)} %bitcast.155), kind=kOutput, calls=%fused_computation.177 | convolution fusion | flops 143007744 | bytes 4671744 | tf_op jit(solution)/shard_map/shqgk,gskhd->shqd/dot_general | solution.py:99
  151.8 15.2 %fusion = bf16[136,1024]{1,0:T(8,128)(2,1)S(1)} fusion(bf16[528,1024]{1,0:T(8,128)(2,1)S(1)} %convolution_convert_fusion.1), kind=kCustom, calls=%all-reduce-scatter | all-reduce-scatter fusion | flops 557057 | bytes 1360384
  172.9 15.6 %all-gather.19.cloned.1.call-done = bf16[4,132,1024]{2,1,0:T(8,128)(2,1)} async-done(((bf16[1,132,1024]{2,1,0:T(8,128)(2,1)}), bf16[4,132,1024]{2,1,0:T(8,128)(2,1)}) %all-gather.19.cloned.1.call-update) | async-done | bytes 1081360 | tf_op jit(solution)/shard_map/all_gather | solution.py:136
  188.5 1.7 reshape.176
  190.2 8.7 %fusion.71 = bf16[528,1024]{1,0:T(8,128)(2,1)S(1)} fusion(bf16[2,1024,1024]{2,1,0:T(8,128)(2,1)} %param.28, f32[1024]{0:T(1024)} %bitcast.168, bf16[528,1024]{1,0:T(8,128)(2,1)S(1)} %reshape.176, bf16[2,1024,1024]{2,1,0:T(8,128)(2,1)} %param.26), kind=kOutput, calls=%fused_computation.96 | convolution fusion | flops 2250817536 | bytes 6361088 | tf_op jit(solution)/shard_map/dot_general | solution.py:144
  199.0 15.4 %fusion.1 = bf16[136,1024]{1,0:T(8,128)(2,1)S(1)} fusion(bf16[528,1024]{1,0:T(8,128)(2,1)S(1)} %fusion.71), kind=kCustom, calls=%all-reduce-scatter.1 | all-reduce-scatter fusion | flops 557057 | bytes 1360384
  217.4 1.6 fusion.199
  219.1 19.4 %all-gather.21.cloned.1.call-done = bf16[4,132,1024]{2,1,0:T(8,128)(2,1)} async-done(((bf16[1,132,1024]{2,1,0:T(8,128)(2,1)}), bf16[4,132,1024]{2,1,0:T(8,128)(2,1)}) %all-gather.21.cloned.1.call-update) | async-done | bytes 1081360 | tf_op jit(solution)/shard_map/all_gather | solution.py:151
  240.6 2.6 fusion.94
  245.3 48.7 %all-gather.15.cloned.1.call-done = bf16[8,8,66,256]{3,1,2,0:T(8,128)(2,1)} async-done(((bf16[1,8,66,256]{3,1,2,0:T(8,128)(2,1)}), bf16[8,8,66,256]{3,1,2,0:T(8,128)(2,1)}) %all-gather.15.cloned.1.call-update) | async-done | bytes 2162704 | tf_op jit(solution)/shard_map/all_gather | solution.py:80
  294.0 7.4 %reshape.172 = bf16[8,8,66,4,64]{4,3,1,2,0:T(4,128)(2,1)} reshape(bf16[8,8,66,256]{3,1,2,0:T(8,128)(2,1)} %all-gather.15.cloned.1.call-done) | data formatting | bytes 4325376 | tf_op jit(solution)/shard_map/reshape | solution.py:89
  301.4 8.7 %fusion.13 = f32[8,4,66,8,66]{2,4,3,1,0:T(8,128)} fusion(bf16[8,8,66,4,64]{4,3,1,2,0:T(4,128)(2,1)} %reshape.172, bf16[8,66,4,64,1]{3,2,1,0,4:T(4,128)(2,1)S(1)} %bitcast.145), kind=kOutput, calls=%fused_computation.13 | convolution fusion | flops 142737408 | bytes 6893568 | tf_op jit(solution)/shard_map/sqhd,gskhd->shqgk/dot_general | solution.py:92
  310.1 10.7 %copy.73 = f32[8,4,66,8,66]{4,3,2,1,0:T(8,128)} copy(f32[8,4,66,8,66]{2,4,3,1,0:T(8,128)} %fusion.13) | data formatting | bytes 8921088 | tf_op jit(solution)/shard_map/sqhd,gskhd->shqgk/dot_general | solution.py:92
  320.8 8.5 %fusion.5 = f32[8,4,66]{2,1,0:T(4,128)S(1)} fusion(f32[8,4,66,8,66]{4,3,2,1,0:T(8,128)} %copy.73, pred[8,66]{1,0:T(8,128)(4,1)S(1)} %copy-done.8), kind=kLoop, calls=%fused_computation.5 | loop fusion | flops 3343296 | bytes 4469520 | tf_op jit(solution)/shard_map/reduce_max | solution.py:96
  329.3 31.2 %fusion.8 = (f32[8,4,66]{2,1,0:T(4,128)S(1)}, bf16[8,4,66,8,66]{4,3,2,1,0:T(8,128)(2,1)}) fusion(f32[8,4,66,8,66]{4,3,2,1,0:T(8,128)S(1)} %copy-done, f32[8,4,66]{2,1,0:T(4,128)S(1)} %broadcast_maximum_fusion, pred[8,66]{1,0:T(8,128)(4,1)S(1)} %copy-done.8), kind=kLoop, calls=%fused_computation.8 | loop fusion | flops 6688704 | bytes 6708240 | tf_op jit(solution)/shard_map/reduce_sum | solution.py:98
  360.5 7.4 %reshape.173 = bf16[8,8,66,4,64]{4,3,1,2,0:T(4,128)(2,1)} reshape(bf16[8,8,66,256]{3,1,2,0:T(8,128)(2,1)} %all-gather.17.cloned.1.call-done) | data formatting | bytes 4325376 | tf_op jit(solution)/shard_map/reshape | solution.py:90
  367.9 8.5 %divide_convert_fusion = bf16[8,66,4,64]{1,3,2,0:T(8,128)(2,1)S(1)} fusion(bf16[8,8,66,4,64]{4,3,1,2,0:T(4,128)(2,1)} %reshape.173, bf16[8,4,66,8,66]{4,3,2,1,0:T(8,128)(2,1)} %get-tuple-element.6, f32[8,66,4]{1,2,0:T(4,128)S(1)} %bitcast.154), kind=kOutput, calls=%fused_computation.176 | convolution fusion | flops 143007744 | bytes 4671744 | tf_op jit(solution)/shard_map/shqgk,gskhd->shqd/dot_general | solution.py:99
  378.1 15.2 %fusion.2 = bf16[136,1024]{1,0:T(8,128)(2,1)S(1)} fusion(bf16[528,1024]{1,0:T(8,128)(2,1)S(1)} %convolution_convert_fusion), kind=kCustom, calls=%all-reduce-scatter.2 | all-reduce-scatter fusion | flops 557057 | bytes 1360384
  397.8 17.4 %all-gather.23.cloned.1.call-done = bf16[4,132,1024]{2,1,0:T(8,128)(2,1)} async-done(((bf16[1,132,1024]{2,1,0:T(8,128)(2,1)}), bf16[4,132,1024]{2,1,0:T(8,128)(2,1)}) %all-gather.23.cloned.1.call-update) | async-done | bytes 1081360 | tf_op jit(solution)/shard_map/all_gather | solution.py:136
  416.5 8.7 %fusion.74 = bf16[528,1024]{1,0:T(8,128)(2,1)S(1)} fusion(bf16[2,1024,1024]{2,1,0:T(8,128)(2,1)} %param.28, f32[1024]{0:T(1024)} %bitcast.166, bf16[528,1024]{1,0:T(8,128)(2,1)S(1)} %reshape.180, bf16[2,1024,1024]{2,1,0:T(8,128)(2,1)} %param.26), kind=kOutput, calls=%fused_computation.97 | convolution fusion | flops 2250817536 | bytes 6361088 | tf_op jit(solution)/shard_map/dot_general | solution.py:144
  425.2 15.4 %fusion.3 = bf16[136,1024]{1,0:T(8,128)(2,1)S(1)} fusion(bf16[528,1024]{1,0:T(8,128)(2,1)S(1)} %fusion.74), kind=kCustom, calls=%all-reduce-scatter.3 | all-reduce-scatter fusion | flops 557057 | bytes 1360384
  443.1 1.7 fusion.201
  (139 shorter events, 31.2 us)
Async XLA Ops:
  6.5 5.1 %copy-start.2 = (bf16[1,528,1024]{2,1,0:T(8,128)(2,1)S(1)}, bf16[1,528,1024]{2,1,0:T(8,128)(2,1)}, u32[]{:S(2)}) copy-start(bf16[1,528,1024]{2,1,0:T(8,128)(2,1)} %param.15) | copy-start | bytes 3244036
  6.5 3.3 copy-start.18
  6.5 3.9 copy-start.12
  6.5 4.5 copy-start.13
  6.5 61.3 %all-gather.11.cloned.1.call-start = ((), (), s32[]{:S(2)}) async-start(), calls=%async_computation | async-start | bytes 2433024 | tf_op jit(solution)/shard_map/all_gather | solution.py:80
  14.3 3.3 copy-start.23
  14.3 4.3 copy-start.14
  14.3 4.9 %copy-start.15 = (f32[2,1024]{1,0:T(2,128)S(1)}, f32[2,1024]{1,0:T(2,128)}, u32[]{:S(2)}) copy-start(f32[2,1024]{1,0:T(2,128)} %param.24) | copy-start | bytes 24580
  15.2 119.0 %all-gather.13.cloned.1.call-start = ((), (), s32[]{:S(2)}) async-start(), calls=%async_computation.1 | async-start | bytes 2433024 | tf_op jit(solution)/shard_map/all_gather | solution.py:81
  16.1 172.4 %all-gather.19.cloned.1.call-start = ((), (), s32[]{:S(2)}) async-start(), calls=%async_computation.4 | async-start | bytes 1392640 | tf_op jit(solution)/shard_map/all_gather | solution.py:136
  18.6 84.4 %copy-start.7 = (pred[8,66]{1,0:T(8,128)(4,1)}, pred[8,66]{1,0:T(8,128)(4,1)S(1)}, u32[]{:S(2)}) copy-start(pred[8,66]{1,0:T(8,128)(4,1)S(1)} %broadcast_and_fusion) | copy-start | bytes 1588
  19.2 151.9 %copy-start.6 = (f32[1,1024]{1,0:T(1,128)}, f32[1,1024]{1,0:T(1,128)S(1)}, u32[]{:S(2)}) copy-start(f32[1,1024]{1,0:T(1,128)S(1)} %get-tuple-element.21) | copy-start | bytes 12292
  94.5 8.5 %copy-start.1 = (f32[8,4,66,8,66]{4,3,2,1,0:T(8,128)S(1)}, f32[8,4,66,8,66]{4,3,2,1,0:T(8,128)}, u32[]{:S(2)}) copy-start(f32[8,4,66,8,66]{4,3,2,1,0:T(8,128)} %copy.65) | copy-start | bytes 13381636
  150.6 17.7 %copy-start.16 = (f32[2,1024]{1,0:T(2,128)S(1)}, f32[2,1024]{1,0:T(2,128)}, u32[]{:S(2)}) copy-start(f32[2,1024]{1,0:T(2,128)} %param.25) | copy-start | bytes 24580
  150.6 18.3 %copy-start.21 = (u32[32]{0:T(128)S(1)}, u32[32]{0:T(128)}, u32[]{:S(2)}) copy-start(u32[32]{0:T(128)} %constant.132) | copy-start | bytes 388
  151.8 20.5 %copy-start.17 = (f32[2,1024]{1,0:T(2,128)S(1)}, f32[2,1024]{1,0:T(2,128)}, u32[]{:S(2)}) copy-start(f32[2,1024]{1,0:T(2,128)} %param.27) | copy-start | bytes 24580
  167.0 3.1 collective-permute-start
  172.2 66.3 %all-gather.21.cloned.1.call-start = ((), (), s32[]{:S(2)}) async-start(), calls=%async_computation.5 | async-start | bytes 1392640 | tf_op jit(solution)/shard_map/all_gather | solution.py:151
  199.0 20.1 %copy-start.11 = (f32[1,3,256]{2,0,1:T(1,128)S(1)}, f32[1,3,256]{2,0,1:T(1,128)}, u32[]{:S(2)}) copy-start(f32[1,3,256]{2,0,1:T(1,128)} %get-tuple-element.29) | copy-start | bytes 9220
  214.4 2.7 collective-permute-start.1
  219.1 75.0 %all-gather.15.cloned.1.call-start = ((), (), s32[]{:S(2)}) async-start(), calls=%async_computation.2 | async-start | bytes 2433024 | tf_op jit(solution)/shard_map/all_gather | solution.py:80
  219.1 21.4 %copy-start.19 = (f32[1,1024]{1,0:T(1,128)S(1)}, f32[1,1024]{1,0:T(1,128)}, u32[]{:S(2)}) copy-start(f32[1,1024]{1,0:T(1,128)} %get-tuple-element.17) | copy-start | bytes 12292
  219.1 21.4 %copy-start.20 = (f32[1,1024]{1,0:T(1,128)S(1)}, f32[1,1024]{1,0:T(1,128)}, u32[]{:S(2)}) copy-start(f32[1,1024]{1,0:T(1,128)} %get-tuple-element.19) | copy-start | bytes 12292
  244.1 116.5 %all-gather.17.cloned.1.call-start = ((), (), s32[]{:S(2)}) async-start(), calls=%async_computation.3 | async-start | bytes 2433024 | tf_op jit(solution)/shard_map/all_gather | solution.py:81
  245.0 170.2 %all-gather.23.cloned.1.call-start = ((), (), s32[]{:S(2)}) async-start(), calls=%async_computation.6 | async-start | bytes 1392640 | tf_op jit(solution)/shard_map/all_gather | solution.py:136
  310.1 10.7 %copy-start.8 = (pred[8,66]{1,0:T(8,128)(4,1)S(1)}, pred[8,66]{1,0:T(8,128)(4,1)}, u32[]{:S(2)}) copy-start(pred[8,66]{1,0:T(8,128)(4,1)} %copy-done.7) | copy-start | bytes 1588
  320.8 8.5 %copy-start = (f32[8,4,66,8,66]{4,3,2,1,0:T(8,128)S(1)}, f32[8,4,66,8,66]{4,3,2,1,0:T(8,128)}, u32[]{:S(2)}) copy-start(f32[8,4,66,8,66]{4,3,2,1,0:T(8,128)} %copy.73) | copy-start | bytes 13381636
  377.6 18.4 %copy-start.5 = (f32[1,1024]{1,0:T(1,128)S(1)}, f32[1,1024]{1,0:T(1,128)}, u32[]{:S(2)}) copy-start(f32[1,1024]{1,0:T(1,128)} %get-tuple-element.22) | copy-start | bytes 12292
  377.6 19.0 %copy-start.9 = (f32[1,1024]{1,0:T(1,128)S(1)}, f32[1,1024]{1,0:T(1,128)}, u32[]{:S(2)}) copy-start(f32[1,1024]{1,0:T(1,128)} %get-tuple-element.24) | copy-start | bytes 12292
  377.6 19.0 %copy-start.10 = (f32[1,1024]{1,0:T(1,128)S(1)}, f32[1,1024]{1,0:T(1,128)}, u32[]{:S(2)}) copy-start(f32[1,1024]{1,0:T(1,128)} %get-tuple-element.26) | copy-start | bytes 12292
  393.3 2.1 collective-permute-start.2
  440.6 2.1 collective-permute-start.3
  (3 other events, 4.8 us)
Sparse Core Ops, SparseCore 0:
  15.3 52.5 all-gather.10
  70.0 48.2 all-gather.12
  172.4 16.1 all-gather.18
  219.2 19.3 all-gather.20
  244.2 49.7 all-gather.14
  296.1 48.4 all-gather.16
  397.9 17.2 all-gather.22
where the time goes:
time: 457 us; the launch traced here: 452 us
  waiting for transfers between devices  151 us (33%)
  other arithmetic  92 us (20%)
  local copies, waits for them, and re-layouts  69.3 us (15%)
  blocking collectives  61.1 us (13%)
  matrix products  57.9 us (13%)
  between operations  15 us (3%)
  starting transfers between devices  5.62 us (1%)
    all_gather x2, waiting for transfers between devices, shards(): key_block = lax.all_gather(keys_mine, 'tm', axis=0, tiled=True)  96.8 us
    reduce_sum x2, other arithmetic, shards(): total_new = jnp.sum(weights, axis=(3, 4))  62.4 us
    unnamed x4, blocking collectives  61.1 us
    all_gather x2, waiting for transfers between devices, shards(): lax.all_gather(normed_two, 'tensor', axis=0, tiled=True)  33 us
    dot_general x2, local copies, waits for them, and re-layouts, shards(): jnp.einsum('sqhd,gskhd->shqgk', queries, keys_split, preferred_element_ty...  21.4 us
    all_gather x1, waiting for transfers between devices, shards(): full_in = lax.all_gather(new_share, 'tensor', axis=0, tiled=True)  19.4 us
    dot_general x2, matrix products, shards(): jnp.dot(inner, fc2_layer, preferred_element_type=jnp.float32)  17.4 us
    dot_general x2, matrix products, shards(): jnp.einsum('sqhd,gskhd->shqgk', queries, keys_split, preferred_element_ty...  17.4 us
  transfers between devices with their start and end apart: 11, of which 7 were waited for; matrix products, arithmetic and copies ran while one was open for 31% of the time, Pallas kernels for 0%

commit v1 on v0

--- a/solution.py
+++ b/solution.py
@@ -29,7 +29,7 @@
     return (piece_time, valid)
 
 
-def shards(
+def shards_gather(
     frames_in,
     frame_time,
     cond_count,
@@ -152,6 +152,133 @@
     return new_share[None]
 
 
+def shards_clip(
+    frames_in,
+    frame_time,
+    cond_count,
+    ln1_gain,
+    ln1_bias,
+    qkv_weight,
+    qkv_bias,
+    out_weight,
+    out_bias,
+    ln2_gain,
+    ln2_bias,
+    fc1_weight,
+    fc1_bias,
+    fc2_weight,
+    fc2_bias,
+):
+    frame_count = frame_time.shape[0]
+    piece_count = lax.axis_size("tm")
+    frame_split = piece_count // frame_count
+    piece_rows = PATCH_DEV + COND // frame_split
+    row_count = frames_in.shape[1]
+    seq_count = row_count // piece_rows
+    clips = seq_count // piece_count
+    head_dim = D // HEADS
+    head_local = qkv_weight.shape[3] // head_dim
+    scale = head_dim ** (-0.5)
+    tensor_size = lax.axis_size("tensor")
+    tensor_pos = lax.axis_index("tensor")
+    share_rows = row_count // tensor_size
+    share_cols = D // tensor_size
+    piece_time, valid = piece_tables(frame_time, cond_count, piece_count, frame_split, piece_rows)
+    row_time = jnp.repeat(piece_time, piece_rows)
+    allowed = (row_time[None, :] <= row_time[:, None]) & valid.reshape(1, -1)
+    clip_rows = piece_count * piece_rows
+    mine = lax.dynamic_slice_in_dim(frames_in[0], tensor_pos * share_cols, share_cols, 1)
+    mine = mine.reshape(piece_count, clips, piece_rows, share_cols)
+    mine = lax.all_to_all(mine, "tm", 0, 0, tiled=True)
+    mine = mine.transpose(1, 0, 2, 3).reshape(row_count, share_cols)
+    full_in = lax.all_gather(mine, "tensor", axis=1, tiled=True)
+    new_share = None
+    for layer_idx in range(LAYERS):
+        normed = layer_norm(
+            full_in.astype(jnp.float32), ln1_gain[layer_idx], ln1_bias[layer_idx]
+        ).astype(jnp.bfloat16)
+        parts = []
+        for i in range(3):
+            part = jnp.dot(normed, qkv_weight[layer_idx, i], preferred_element_type=jnp.float32)
+            part = (part + qkv_bias[layer_idx, i]).astype(jnp.bfloat16)
+            parts.append(part.reshape(clips, clip_rows, head_local, head_dim))
+        queries, keys, values = parts
+        scores = (
+            jnp.einsum("sqhd,skhd->shqk", queries, keys, preferred_element_type=jnp.float32) * scale
+        )
+        scores = jnp.where(allowed, scores, -1e30)
+        top = jnp.max(scores, axis=-1, keepdims=True)
+        weights = jnp.where(allowed, jnp.exp(scores - top), 0.0)
+        total = jnp.sum(weights, axis=-1, keepdims=True)
+        mixed = jnp.einsum(
+            "shqk,skhd->shqd",
+            weights.astype(jnp.bfloat16),
+            values,
+            preferred_element_type=jnp.float32,
+        )
+        attended = (
+            (mixed / total)
+            .transpose(0, 2, 1, 3)
+            .reshape(row_count, head_local * head_dim)
+            .astype(jnp.bfloat16)
+        )
+        own_rows = lax.dynamic_slice_in_dim(full_in, tensor_pos * share_rows, share_rows, 0).astype(
+            jnp.float32
+        )
+        first = (
+            own_rows
+            + lax.psum_scatter(
+                jnp.dot(
+                    attended, out_weight[layer_idx], preferred_element_type=jnp.float32
+                ).astype(jnp.bfloat16),
+                "tensor",
+                scatter_dimension=0,
+                tiled=True,
+            ).astype(jnp.float32)
+            + out_bias[layer_idx]
+        )
+        normed_two = layer_norm(first, ln2_gain[layer_idx], ln2_bias[layer_idx]).astype(
+            jnp.bfloat16
+        )
+        inner = jax.nn.gelu(
+            jnp.dot(
+                lax.all_gather(normed_two, "tensor", axis=0, tiled=True),
+                fc1_weight[layer_idx],
+                preferred_element_type=jnp.float32,
+            )
+            + fc1_bias[layer_idx],
+            approximate=False,
+        ).astype(jnp.bfloat16)
+        mlp_share = lax.psum_scatter(
+            jnp.dot(inner, fc2_weight[layer_idx], preferred_element_type=jnp.float32).astype(
+                jnp.bfloat16
+            ),
+            "tensor",
+            scatter_dimension=0,
+            tiled=True,
+        ).astype(jnp.float32)
+        new_share = (first + mlp_share + fc2_bias[layer_idx]).astype(jnp.bfloat16)
+        if layer_idx + 1 < LAYERS:
+            full_in = lax.all_gather(new_share, "tensor", axis=0, tiled=True)
+    cols = jnp.stack(jnp.split(new_share, tensor_size, axis=1))
+    cols = lax.all_to_all(cols, "tensor", 0, 0, tiled=True)
+    cols = cols.reshape(clips, piece_count, piece_rows, share_cols).transpose(1, 0, 2, 3)
+    cols = lax.all_to_all(cols, "tm", 0, 0, tiled=True)
+    cols = cols.reshape(tensor_size, share_rows, share_cols)
+    cols = lax.all_to_all(cols, "tensor", 0, 0, tiled=True)
+    out = cols.transpose(1, 0, 2).reshape(share_rows, D)
+    return out[None]
+
+
+def shards(frames_in, frame_time, cond_count, *rest):
+    frame_split = lax.axis_size("tm") // frame_time.shape[0]
+    piece_rows = PATCH_DEV + COND // frame_split
+    seq_count = frames_in.shape[1] // piece_rows
+    by_clip = seq_count % lax.axis_size("tm") == 0
+    body = shards_clip if by_clip else shards_gather
+    return body(frames_in, frame_time, cond_count, *rest)
+
+
 def solution(mesh):
     in_specs = (
         P("tm", None, None),

time: 457 us -> 283 us (0.62)
  other arithmetic: 92 us -> 13.4 us
  waiting for transfers between devices: 151 us -> 78.6 us
  local copies, waits for them, and re-layouts: 69.3 us -> 19.8 us
  blocking collectives: 61.1 us -> 97.6 us
  matrix products: 57.9 us -> 45.1 us
  starting transfers between devices: 5.62 us -> 13.3 us
    all_gather x7 -> x4, waiting for transfers between devices: 149 us -> 69.1 us  [the longest x2 38.1 us: shards_clip(): lax.all_gather(normed_two, 'tensor', axis=0, tiled=True)]
    reduce_sum x4 -> x0, other arithmetic: 63.3 us -> none  [the longest x2 62.4 us: shards(): total_new = jnp.sum(weights, axis=(3, 4))]
    all_to_all x0 -> x3, blocking collectives: none -> 35 us  [the longest x2 19.2 us: shards_clip(): cols = lax.all_to_all(cols, 'tensor', 0, 0, tiled=True)]
    reshape x4 -> x2, local copies, waits for them, and re-layouts: 29.3 us -> 0.84 us  [the longest x1 0.78 us: shards_clip(): mine = mine.reshape(piece_count, clips, piece_rows, share_cols)]
    dot_general x10 -> x12, matrix products: 57.9 us -> 34.3 us  [the longest x2 19.5 us: shards_clip(): jnp.dot(inner, fc2_weight[layer_idx], preferred_element_type=jnp.float32)]
    dot_general x2 -> x0, local copies, waits for them, and re-layouts: 21.4 us -> none  [shards(): jnp.einsum('sqhd,gskhd->shqgk', queries, keys_split, preferred_element_ty...]
    reduce_max x2 -> x0, other arithmetic: 17 us -> none  [shards(): new_top = jnp.maximum(top_run, jnp.max(scores, axis=(3, 4)))]
    sub x0 -> x2, matrix products: none -> 10.8 us  [shards_clip(): weights = jnp.where(allowed, jnp.exp(scores - top), 0.0)]
  transfers between devices with their start and end apart: 11 -> 9, of which waited for: 7 -> 7; matrix products, arithmetic and copies ran while one was open for 31% -> 3% of each run, Pallas kernels for 0% -> 0%
where the time goes in v1:
time: 283 us; the launch traced here: 282 us
  blocking collectives  97.6 us (34%)
  waiting for transfers between devices  78.6 us (28%)
  matrix products  45.1 us (16%)
  local copies, waits for them, and re-layouts  19.8 us (7%)
  between operations  14.3 us (5%)
  other arithmetic  13.4 us (5%)
  starting transfers between devices  13.3 us (5%)
    unnamed x4, blocking collectives  62.5 us
    all_gather x2, waiting for transfers between devices, shards_clip(): lax.all_gather(normed_two, 'tensor', axis=0, tiled=True)  38.1 us
    dot_general x2, matrix products, shards_clip(): jnp.dot(inner, fc2_weight[layer_idx], preferred_element_type=jnp.float32)  19.5 us
    all_gather x1, waiting for transfers between devices, shards_clip(): full_in = lax.all_gather(new_share, 'tensor', axis=0, tiled=True)  19.2 us
    all_to_all x2, blocking collectives, shards_clip(): cols = lax.all_to_all(cols, 'tensor', 0, 0, tiled=True)  19.2 us
    all_to_all x1, blocking collectives, shards_clip(): cols = lax.all_to_all(cols, 'tm', 0, 0, tiled=True)  15.8 us
    all_gather x1, waiting for transfers between devices, shards_clip(): full_in = lax.all_gather(mine, 'tensor', axis=1, tiled=True)  11.8 us
    sub x2, matrix products, shards_clip(): weights = jnp.where(allowed, jnp.exp(scores - top), 0.0)  10.8 us
  transfers between devices with their start and end apart: 9, of which 7 were waited for; matrix products, arithmetic and copies ran while one was open for 3% of the time, Pallas kernels for 0%

profile of v1, /device:TPU:0, one launch (start us, length us, event | category | flops | bytes accessed | tf_op | source)
XLA Modules:
  0.0 282.2 jit_solution(10008635543005344850)
XLA Ops:
  8.6 7.3 %all-to-all-start = ((bf16[8,1,66,256]{3,2,1,0:T(8,128)(2,1)}), bf16[8,1,66,256]{3,2,1,0:T(8,128)(2,1)S(1)}, u32[]{:S(2)}, u32[]{:S(2)}) async-start(bf16[8,1,66,256]{3,2,1,0:T(8,128)(2,1)} %bitcast), calls=%async_computation | async-start | bytes 589824 | tf_op jit(solution)/shard_map/all_to_all | solution.py:192
  17.5 8.0 %all-to-all-done = bf16[8,1,66,256]{3,2,1,0:T(8,128)(2,1)S(1)} async-done(((bf16[8,1,66,256]{3,2,1,0:T(8,128)(2,1)}), bf16[8,1,66,256]{3,2,1,0:T(8,128)(2,1)S(1)}, u32[]{:S(2)}, u32[]{:S(2)}) %all-to-all-start) | async-done | bytes 270368 | tf_op jit(solution)/shard_map/all_to_all | solution.py:192
  30.8 11.8 %all-gather.8.cloned.1.call-done = bf16[528,1024]{1,0:T(8,128)(2,1)} async-done(((bf16[528,256]{1,0:T(8,128)(2,1)}), bf16[528,1024]{1,0:T(8,128)(2,1)}) %all-gather.8.cloned.1.call-update) | async-done | bytes 1081360 | tf_op jit(solution)/shard_map/all_gather | solution.py:194
  42.5 1.6 convert_reduce_fusion.1
  44.1 1.7 fusion.26
  46.2 1.5 fusion.82
  48.7 1.5 fusion.80
  51.0 1.5 fusion.81
  52.8 5.4 %fusion.256 = (f32[4,528]{1,0:T(4,128)S(1)}, bf16[4,528,528]{1,2,0:T(8,128)(2,1)}) fusion(pred[528,528]{0,1:T(8,128)(4,1)} %compare_and_fusion, bf16[528,4,64]{0,2,1:T(8,128)(2,1)} %bitcast.137, bf16[528,4,64]{0,2,1:T(8,128)(2,1)S(1)} %bitcast.139), kind=kOutput, calls=%fused_computation.290 | convolution fusion | flops 149428752 | bytes 3058176 | tf_op jit(solution)/shard_map/sub | solution.py:211
  58.2 2.5 fusion.77
  61.2 15.4 %fusion = bf16[136,1024]{1,0:T(8,128)(2,1)S(1)} fusion(bf16[528,1024]{1,0:T(8,128)(2,1)S(1)} %convolution_convert_fusion.1), kind=kCustom, calls=%all-reduce-scatter | all-reduce-scatter fusion | flops 557057 | bytes 1360384
  82.6 18.1 %all-gather.10.cloned.1.call-done = bf16[4,132,1024]{2,1,0:T(8,128)(2,1)} async-done(((bf16[1,132,1024]{2,1,0:T(8,128)(2,1)}), bf16[4,132,1024]{2,1,0:T(8,128)(2,1)}) %all-gather.10.cloned.1.call-update) | async-done | bytes 1081360 | tf_op jit(solution)/shard_map/all_gather | solution.py:245
  100.7 1.3 reshape.189
  102.1 9.7 %fusion.62 = bf16[528,1024]{1,0:T(8,128)(2,1)} fusion(bf16[2,1024,1024]{2,1,0:T(8,128)(2,1)} %param.28, f32[1024]{0:T(1024)} %bitcast.161, bf16[528,1024]{1,0:T(8,128)(2,1)S(1)} %reshape.189, bf16[2,1024,1024]{2,1,0:T(8,128)(2,1)} %param.26), kind=kOutput, calls=%fused_computation.84 | convolution fusion | flops 2250817536 | bytes 6361088 | tf_op jit(solution)/shard_map/dot_general | solution.py:253
  111.8 15.9 %fusion.1 = bf16[136,1024]{1,0:T(8,128)(2,1)S(1)} fusion(bf16[528,1024]{1,0:T(8,128)(2,1)} %fusion.62), kind=kCustom, calls=%all-reduce-scatter.1 | all-reduce-scatter fusion | flops 557057 | bytes 1360384
  129.0 1.4 fusion.248
  130.7 1.6 fusion.181
  132.7 19.2 %all-gather.12.cloned.1.call-done = bf16[4,132,1024]{2,1,0:T(8,128)(2,1)} async-done(((bf16[1,132,1024]{2,1,0:T(8,128)(2,1)}), bf16[4,132,1024]{2,1,0:T(8,128)(2,1)}) %all-gather.12.cloned.1.call-update) | async-done | bytes 1081360 | tf_op jit(solution)/shard_map/all_gather | solution.py:262
  151.9 1.3 reshape.191
  154.5 1.5 fusion.85
  156.9 1.5 fusion.83
  159.3 1.5 fusion.84
  161.0 5.4 %fusion.257 = (f32[4,528]{1,0:T(4,128)S(1)}, bf16[4,528,528]{1,2,0:T(8,128)(2,1)}) fusion(pred[528,528]{0,1:T(8,128)(4,1)} %compare_and_fusion, bf16[528,4,64]{0,2,1:T(8,128)(2,1)} %bitcast.136, bf16[528,4,64]{0,2,1:T(8,128)(2,1)S(1)} %bitcast.138), kind=kOutput, calls=%fused_computation.291 | convolution fusion | flops 149428752 | bytes 3058176 | tf_op jit(solution)/shard_map/sub | solution.py:211
  166.4 2.5 fusion.74
  169.4 15.4 %fusion.2 = bf16[136,1024]{1,0:T(8,128)(2,1)S(1)} fusion(bf16[528,1024]{1,0:T(8,128)(2,1)S(1)} %convolution_convert_fusion), kind=kCustom, calls=%all-reduce-scatter.2 | all-reduce-scatter fusion | flops 557057 | bytes 1360384
  184.8 1.6 collective-permute-start.2
  189.0 20.0 %all-gather.14.cloned.1.call-done = bf16[4,132,1024]{2,1,0:T(8,128)(2,1)} async-done(((bf16[1,132,1024]{2,1,0:T(8,128)(2,1)}), bf16[4,132,1024]{2,1,0:T(8,128)(2,1)}) %all-gather.14.cloned.1.call-update) | async-done | bytes 1081360 | tf_op jit(solution)/shard_map/all_gather | solution.py:245
  210.3 9.7 %fusion.65 = bf16[528,1024]{1,0:T(8,128)(2,1)} fusion(bf16[2,1024,1024]{2,1,0:T(8,128)(2,1)} %param.28, f32[1024]{0:T(1024)} %bitcast.160, bf16[528,1024]{1,0:T(8,128)(2,1)S(1)} %reshape.193, bf16[2,1024,1024]{2,1,0:T(8,128)(2,1)} %param.26), kind=kOutput, calls=%fused_computation.85 | convolution fusion | flops 2250817536 | bytes 6361088 | tf_op jit(solution)/shard_map/dot_general | solution.py:253
  220.1 15.9 %fusion.3 = bf16[136,1024]{1,0:T(8,128)(2,1)S(1)} fusion(bf16[528,1024]{1,0:T(8,128)(2,1)} %fusion.65), kind=kCustom, calls=%all-reduce-scatter.3 | all-reduce-scatter fusion | flops 557057 | bytes 1360384
  239.5 10.7 %all_to_all.20 = bf16[4,132,256]{2,1,0:T(8,128)(2,1)S(1)} all-to-all(bf16[4,132,256]{2,1,0:T(8,128)(2,1)S(1)} %pad_maximum_fusion), channel_id=1, replica_groups=mesh['tm'=8,'tensor'=4] {'tensor'}, dimensions={0} | all-to-all | bytes 540672 | tf_op jit(solution)/shard_map/all_to_all | solution.py:264
  250.2 15.8 %all_to_all.21 = bf16[8,1,66,256]{3,2,1,0:T(8,128)(2,1)S(1)} all-to-all(bf16[8,1,66,256]{3,2,1,0:T(8,128)(2,1)S(1)} %bitcast.132), channel_id=1, replica_groups=mesh['tm'=8,'tensor'=4] {'tm'}, dimensions={0} | all-to-all | bytes 540672 | tf_op jit(solution)/shard_map/all_to_all | solution.py:266
  266.1 8.5 %all_to_all.22 = bf16[4,132,256]{2,1,0:T(8,128)(2,1)S(1)} all-to-all(bf16[4,132,256]{2,1,0:T(8,128)(2,1)S(1)} %reshape.187), channel_id=1, replica_groups=mesh['tm'=8,'tensor'=4] {'tensor'}, dimensions={0} | all-to-all | bytes 540672 | tf_op jit(solution)/shard_map/all_to_all | solution.py:268
  (122 shorter events, 31.2 us)
Async XLA Ops:
  6.5 1.2 copy-start
  6.5 20.2 %copy-start.18 = (f32[2,3,256]{2,0,1:T(2,128)S(1)}, f32[2,3,256]{2,0,1:T(2,128)}, u32[]{:S(2)}) copy-start(f32[2,3,256]{2,0,1:T(2,128)} %param.21) | copy-start | bytes 18436
  6.5 20.8 %copy-start.12 = (f32[2,1024]{1,0:T(2,128)S(1)}, f32[2,1024]{1,0:T(2,128)}, u32[]{:S(2)}) copy-start(f32[2,1024]{1,0:T(2,128)} %param.25) | copy-start | bytes 24580
  6.5 21.4 %copy-start.13 = (f32[2,1024]{1,0:T(2,128)S(1)}, f32[2,1024]{1,0:T(2,128)}, u32[]{:S(2)}) copy-start(f32[2,1024]{1,0:T(2,128)} %param.24) | copy-start | bytes 24580
  6.5 22.0 %copy-start.14 = (f32[2,1024]{1,0:T(2,128)S(1)}, f32[2,1024]{1,0:T(2,128)}, u32[]{:S(2)}) copy-start(f32[2,1024]{1,0:T(2,128)} %param.19) | copy-start | bytes 24580
  6.5 22.6 %copy-start.15 = (f32[2,1024]{1,0:T(2,128)S(1)}, f32[2,1024]{1,0:T(2,128)}, u32[]{:S(2)}) copy-start(f32[2,1024]{1,0:T(2,128)} %param.18) | copy-start | bytes 24580
  8.6 16.9 %all-to-all-start = ((bf16[8,1,66,256]{3,2,1,0:T(8,128)(2,1)}), bf16[8,1,66,256]{3,2,1,0:T(8,128)(2,1)S(1)}, u32[]{:S(2)}, u32[]{:S(2)}) async-start(bf16[8,1,66,256]{3,2,1,0:T(8,128)(2,1)} %bitcast), calls=%async_computation | async-start | bytes 589824 | tf_op jit(solution)/shard_map/all_to_all | solution.py:192
  15.9 26.6 %all-gather.8.cloned.1.call-start = ((), (), s32[]{:S(2)}) async-start(), calls=%async_computation.4 | async-start | bytes 1351680 | tf_op jit(solution)/shard_map/all_gather | solution.py:194
  26.3 74.4 %all-gather.10.cloned.1.call-start = ((), (), s32[]{:S(2)}) async-start(), calls=%async_computation.5 | async-start | bytes 1392640 | tf_op jit(solution)/shard_map/all_gather | solution.py:245
  42.5 3.3 %copy-start.1 = (bf16[528,1024]{1,0:T(8,128)(2,1)S(1)}, bf16[528,1024]{1,0:T(8,128)(2,1)}, u32[]{:S(2)}) copy-start(bf16[528,1024]{1,0:T(8,128)(2,1)} %all-gather.8.cloned.1.call-done) | copy-start | bytes 3244036
  52.7 5.4 %copy-start.5 = (bf16[528,256]{0,1:T(8,128)(2,1)S(1)}, bf16[528,256]{0,1:T(8,128)(2,1)}, u32[]{:S(2)}) copy-start(bf16[528,256]{0,1:T(8,128)(2,1)} %copy.56) | copy-start | bytes 811012
  58.2 2.5 copy-start.2
  60.7 17.2 %copy-start.16 = (f32[2,1024]{1,0:T(2,128)S(1)}, f32[2,1024]{1,0:T(2,128)}, u32[]{:S(2)}) copy-start(f32[2,1024]{1,0:T(2,128)} %param.23) | copy-start | bytes 24580
  60.7 17.8 %copy-start.22 = (u32[32]{0:T(128)S(1)}, u32[32]{0:T(128)}, u32[]{:S(2)}) copy-start(u32[32]{0:T(128)} %constant.128) | copy-start | bytes 388
  61.2 20.8 %copy-start.17 = (f32[2,1024]{1,0:T(2,128)S(1)}, f32[2,1024]{1,0:T(2,128)}, u32[]{:S(2)}) copy-start(f32[2,1024]{1,0:T(2,128)} %param.27) | copy-start | bytes 24580
  76.6 3.1 %collective-permute-start = (bf16[12,1024]{1,0:T(8,128)(2,1)S(1)}, bf16[12,1024]{1,0:T(8,128)(2,1)S(1)}, u32[]{:S(2)}, u32[]{:S(2)}) collective-permute-start(bf16[12,1024]{1,0:T(8,128)(2,1)S(1)} %slice.128), channel_id=1, source_target_pairs={{0,1},{1,2},{2,3},{4,5},{5,6},{6,7},{8,9},{9,10},{10,11},{12,13},{... | collective-permute-start | bytes 73736
  78.5 4.1 %copy-start.7 = (f32[1,1024]{1,0:T(1,128)}, f32[1,1024]{1,0:T(1,128)S(1)}, u32[]{:S(2)}) copy-start(f32[1,1024]{1,0:T(1,128)S(1)} %get-tuple-element.15) | copy-start | bytes 12292
  81.8 70.1 %all-gather.12.cloned.1.call-start = ((), (), s32[]{:S(2)}) async-start(), calls=%async_computation.6 | async-start | bytes 1392640 | tf_op jit(solution)/shard_map/all_gather | solution.py:262
  127.7 2.7 collective-permute-start.1
  132.4 21.6 %copy-start.10 = (f32[1,1024]{1,0:T(1,128)S(1)}, f32[1,1024]{1,0:T(1,128)}, u32[]{:S(2)}) copy-start(f32[1,1024]{1,0:T(1,128)} %get-tuple-element.13) | copy-start | bytes 12292
  132.4 21.6 %copy-start.11 = (f32[1,1024]{1,0:T(1,128)S(1)}, f32[1,1024]{1,0:T(1,128)}, u32[]{:S(2)}) copy-start(f32[1,1024]{1,0:T(1,128)} %get-tuple-element.11) | copy-start | bytes 12292
  132.4 76.6 %all-gather.14.cloned.1.call-start = ((), (), s32[]{:S(2)}) async-start(), calls=%async_computation.7 | async-start | bytes 1392640 | tf_op jit(solution)/shard_map/all_gather | solution.py:245
  153.3 1.2 copy-start.21
  154.0 2.9 %copy-start.20 = (f32[1,1,256]{2,0,1:T(1,128)S(1)}, f32[1,1,256]{2,0,1:T(1,128)}, u32[]{:S(2)}) copy-start(f32[1,1,256]{2,0,1:T(1,128)} %get-tuple-element.24) | copy-start | bytes 3076
  156.0 3.3 %copy-start.19 = (f32[1,1,256]{2,0,1:T(1,128)S(1)}, f32[1,1,256]{2,0,1:T(1,128)}, u32[]{:S(2)}) copy-start(f32[1,1,256]{2,0,1:T(1,128)} %get-tuple-element.23) | copy-start | bytes 3076
  161.0 5.4 %copy-start.4 = (bf16[528,256]{0,1:T(8,128)(2,1)S(1)}, bf16[528,256]{0,1:T(8,128)(2,1)}, u32[]{:S(2)}) copy-start(bf16[528,256]{0,1:T(8,128)(2,1)} %copy.60) | copy-start | bytes 811012
  166.4 2.5 copy-start.3
  168.9 18.4 %copy-start.6 = (f32[1,1024]{1,0:T(1,128)S(1)}, f32[1,1024]{1,0:T(1,128)}, u32[]{:S(2)}) copy-start(f32[1,1024]{1,0:T(1,128)} %get-tuple-element.16) | copy-start | bytes 12292
  169.0 18.9 %copy-start.8 = (f32[1,1024]{1,0:T(1,128)S(1)}, f32[1,1024]{1,0:T(1,128)}, u32[]{:S(2)}) copy-start(f32[1,1024]{1,0:T(1,128)} %get-tuple-element.20) | copy-start | bytes 12292
  169.0 18.9 %copy-start.9 = (f32[1,1024]{1,0:T(1,128)S(1)}, f32[1,1024]{1,0:T(1,128)}, u32[]{:S(2)}) copy-start(f32[1,1024]{1,0:T(1,128)} %get-tuple-element.18) | copy-start | bytes 12292
  184.8 2.1 collective-permute-start.2
  236.0 2.1 collective-permute-start.3
Sparse Core Ops, SparseCore 0:
  26.4 16.0 all-gather.7
  81.9 18.7 all-gather.9
  132.5 19.3 all-gather.11
  189.1 19.8 all-gather.13

commit v2 on v0

--- a/solution.py
+++ b/solution.py
@@ -1,6 +1,8 @@
 import jax
 import jax.numpy as jnp
 from jax import lax
+from jax.experimental import pallas as pl
+from jax.experimental.pallas import tpu as pltpu
 from jax.sharding import PartitionSpec as P
 
 D = 1024
@@ -29,7 +31,7 @@
     return (piece_time, valid)
 
 
-def shards(
+def shards_gather(
     frames_in,
     frame_time,
     cond_count,
@@ -152,6 +154,285 @@
     return new_share[None]
 
 
+MESH = pl.DeviceIdType.MESH
+
+
+def layers_kernel(
+    share_ref, qt_ref, kt_ref, g1, b1, qkvb, ob, g2, b2, f1b, f2b, wqkv_h, wo_h, w1_h, w2_h,
+    out_ref, wqkv, wo, w1, w2, ag1, ag2, qb, kb, vb, inner, xs, keep, keep_x, stage, rbuf,
+    wsem, ssem, rsem,
+):
+    share = share_ref.shape[0]
+    head_dim = D // HEADS
+    width = qb.shape[1]
+    head_local = width // head_dim
+    me = lax.axis_index("tensor")
+    partner = me + 1 - 2 * (me % 2)
+    across = (me + 2) % 4
+    diagonal = (partner + 2) % 4
+
+    pairs = ((wqkv_h, wqkv), (wo_h, wo), (w1_h, w1), (w2_h, w2))
+
+    def weight_copy(l, j):
+        return pltpu.make_async_copy(pairs[j][0].at[l], pairs[j][1].at[l], wsem.at[l, j])
+
+    for l in range(LAYERS):
+        for j in range(4):
+            weight_copy(l, j).start()
+
+    barrier = pltpu.get_barrier_semaphore()
+    for other in (partner, across, diagonal):
+        pl.semaphore_signal(barrier, inc=1, device_id={"tensor": other}, device_id_type=MESH)
+    pl.semaphore_wait(barrier, 3)
+
+    def rows(s):
+        return pl.ds(pl.multiple_of(s * share, 16), share)
+
+    def send(src, dst, l, j, target):
+        copy = pltpu.make_async_remote_copy(
+            src_ref=src,
+            dst_ref=dst,
+            send_sem=ssem.at[l, j],
+            recv_sem=rsem.at[l, j],
+            device_id={"tensor": target},
+            device_id_type=MESH,
+        )
+        copy.start()
+        return copy
+
+    def gather(buf, l, j, use):
+        own = buf.at[l, rows(me)]
+        to_x = send(own, own, l, j, across)
+        to_p = send(own, own, l, j + 1, partner)
+        use(0, me)
+        to_p.wait_recv()
+        use(1, partner)
+        to_x.wait_recv()
+        got = buf.at[l, rows(across)]
+        fwd = send(got, got, l, j + 2, partner)
+        use(2, across)
+        fwd.wait_recv()
+        use(3, diagonal)
+        to_x.wait_send()
+        to_p.wait_send()
+        fwd.wait_send()
+
+    def norm(x, gain, bias):
+        return layer_norm(x, gain, bias).astype(jnp.bfloat16)
+
+    lane = lax.broadcasted_iota(jnp.int32, (1, width), 1)
+
+    def layer(l, carry):
+        ag1[l, rows(me)] = norm(xs[...], g1[l], b1[l])
+        weight_copy(l, 0).wait()
+
+        def project(step, s):
+            normed = ag1[l, rows(s)]
+            for i, dst in enumerate((qb, kb, vb)):
+                y = jnp.dot(normed, wqkv[l, i], preferred_element_type=jnp.float32) + qkvb[l, i]
+                if i == 0:
+                    y = y * head_dim ** (-0.5)
+                dst[rows(s)] = y.astype(jnp.bfloat16)
+
+        gather(ag1, l, 0, project)
+        weight_copy(l, 1).wait()
+
+        def attend(s):
+            q = qb[rows(s)]
+            allowed = kt_ref[...] <= qt_ref[rows(s)]
+            acc = jnp.zeros((share, width), jnp.float32)
+            for h in range(head_local):
+                mine = (lane >= h * head_dim) & (lane < (h + 1) * head_dim)
+                qm = q * jnp.where(mine, 1.0, 0.0).astype(jnp.bfloat16)
+                sc = lax.dot_general(
+                    qm, kb[...], (((1,), (1,)), ((), ())), preferred_element_type=jnp.float32
+                )
+                sc = jnp.where(allowed, sc, -1e30)
+                w = jnp.exp(sc - jnp.max(sc, axis=-1, keepdims=True))
+                total = jnp.sum(w, axis=-1, keepdims=True)
+                pv = jnp.dot(w.astype(jnp.bfloat16), vb[...], preferred_element_type=jnp.float32)
+                acc = jnp.where(mine, pv / total, acc)
+            return jnp.dot(
+                acc.astype(jnp.bfloat16), wo[l], preferred_element_type=jnp.float32
+            )
+
+        stage[0] = attend(diagonal).astype(jnp.bfloat16)
+        c_f = send(stage.at[0], rbuf.at[l, 0], l, 3, partner)
+        part = attend(across)
+        c_f.wait_recv()
+        stage[1] = (part + rbuf[l, 0].astype(jnp.float32)).astype(jnp.bfloat16)
+        c_x = send(stage.at[1], rbuf.at[l, 1], l, 4, across)
+        stage[2] = attend(partner).astype(jnp.bfloat16)
+        c_p = send(stage.at[2], rbuf.at[l, 2], l, 5, partner)
+        part = attend(me) + xs[...] + ob[l]
+        c_p.wait_recv()
+        part = part + rbuf[l, 2].astype(jnp.float32)
+        c_x.wait_recv()
+        first = part + rbuf[l, 1].astype(jnp.float32)
+        xs[...] = first
+        ag2[l, rows(me)] = norm(first, g2[l], b2[l])
+        c_f.wait_send()
+        c_x.wait_send()
+        c_p.wait_send()
+        weight_copy(l, 2).wait()
+        weight_copy(l, 3).wait()
+
+        def mlp(s):
+            normed = ag2[l, rows(s)]
+            tile = 256
+            for n in range(w1.shape[2] // tile):
+                at = pl.ds(n * tile, tile)
+                y = jnp.dot(normed, w1[l, :, at], preferred_element_type=jnp.float32) + f1b[l, :, at]
+                y = 0.5 * y * (1.0 + lax.erf(y * (0.5**0.5)))
+                inner[:, at] = y.astype(jnp.bfloat16)
+            return jnp.dot(inner[...], w2[l], preferred_element_type=jnp.float32)
+
+        copies = []
+
+        def feed(step, s):
+            part = mlp(s)
+            if step == 0:
+                keep[...] = part
+            elif step == 1:
+                stage[2] = part.astype(jnp.bfloat16)
+                copies.append(send(stage.at[2], rbuf.at[l, 5], l, 11, partner))
+            elif step == 2:
+                keep_x[...] = part
+            else:
+                stage[0] = part.astype(jnp.bfloat16)
+                copies.append(send(stage.at[0], rbuf.at[l, 3], l, 9, partner))
+
+        gather(ag2, l, 6, feed)
+        c_p, c_f = copies
+        c_f.wait_recv()
+        stage[1] = (keep_x[...] + rbuf[l, 3].astype(jnp.float32)).astype(jnp.bfloat16)
+        c_x = send(stage.at[1], rbuf.at[l, 4], l, 10, across)
+        c_p.wait_recv()
+        part = keep[...] + xs[...] + f2b[l] + rbuf[l, 5].astype(jnp.float32)
+        c_x.wait_recv()
+        new = (part + rbuf[l, 4].astype(jnp.float32)).astype(jnp.bfloat16)
+        xs[...] = new.astype(jnp.float32)
+        c_p.wait_send()
+        c_f.wait_send()
+        c_x.wait_send()
+        return carry
+
+    xs[...] = share_ref[...].astype(jnp.float32)
+    lax.fori_loop(0, LAYERS, layer, 0)
+    out_ref[...] = xs[...].astype(jnp.bfloat16)
+
+
+def shards_clip(
+    frames_in,
+    frame_time,
+    cond_count,
+    ln1_gain,
+    ln1_bias,
+    qkv_weight,
+    qkv_bias,
+    out_weight,
+    out_bias,
+    ln2_gain,
+    ln2_bias,
+    fc1_weight,
+    fc1_bias,
+    fc2_weight,
+    fc2_bias,
+):
+    piece_count = lax.axis_size("tm")
+    frame_split = piece_count // frame_time.shape[0]
+    piece_rows = PATCH_DEV + COND // frame_split
+    row_count = frames_in.shape[1]
+    width = qkv_weight.shape[3]
+    hidden = fc1_weight.shape[2]
+    tensor_size = lax.axis_size("tensor")
+    tensor_pos = lax.axis_index("tensor")
+    share_rows = row_count // tensor_size
+    share_cols = D // tensor_size
+    share_pad = -(-share_rows // 16) * 16
+    all_rows = share_pad * tensor_size
+    piece_time, valid = piece_tables(frame_time, cond_count, piece_count, frame_split, piece_rows)
+    far = jnp.int32(1 << 30)
+    row_time = jnp.repeat(piece_time, piece_rows).reshape(tensor_size, share_rows)
+    key_time = jnp.where(valid.reshape(tensor_size, share_rows), row_time, far)
+    pad = ((0, 0), (0, share_pad - share_rows))
+    row_time = jnp.pad(row_time, pad, constant_values=1 << 29).reshape(all_rows, 1)
+    key_time = jnp.pad(key_time, pad, constant_values=1 << 30).reshape(1, all_rows)
+    cols = lax.dynamic_slice_in_dim(frames_in[0], tensor_pos * share_cols, share_cols, 1)
+    cols = cols.reshape(piece_count, piece_rows, share_cols)
+    cols = lax.all_to_all(cols, "tm", 0, 0, tiled=True)
+    cols = cols.reshape(tensor_size, share_rows, share_cols)
+    cols = lax.all_to_all(cols, "tensor", 0, 0, tiled=True)
+    share = cols.transpose(1, 0, 2).reshape(share_rows, D)
+    share = jnp.pad(share, ((0, share_pad - share_rows), (0, 0)))
+
+    vmem = pl.BlockSpec(memory_space=pltpu.VMEM)
+    hbm = pl.BlockSpec(memory_space=pl.ANY)
+    bf16, f32 = jnp.bfloat16, jnp.float32
+    new_share = pl.pallas_call(
+        layers_kernel,
+        out_shape=jax.ShapeDtypeStruct((share_pad, D), bf16),
+        in_specs=[vmem] * 11 + [hbm] * 4,
+        out_specs=vmem,
+        scratch_shapes=[
+            pltpu.VMEM(qkv_weight.shape, bf16),
+            pltpu.VMEM(out_weight.shape, bf16),
+            pltpu.VMEM(fc1_weight.shape, bf16),
+            pltpu.VMEM(fc2_weight.shape, bf16),
+            pltpu.VMEM((LAYERS, all_rows, D), bf16),
+            pltpu.VMEM((LAYERS, all_rows, D), bf16),
+            pltpu.VMEM((all_rows, width), bf16),
+            pltpu.VMEM((all_rows, width), bf16),
+            pltpu.VMEM((all_rows, width), bf16),
+            pltpu.VMEM((share_pad, hidden), bf16),
+            pltpu.VMEM((share_pad, D), f32),
+            pltpu.VMEM((share_pad, D), f32),
+            pltpu.VMEM((share_pad, D), f32),
+            pltpu.VMEM((3, share_pad, D), bf16),
+            pltpu.VMEM((LAYERS, 6, share_pad, D), bf16),
+            pltpu.SemaphoreType.DMA((LAYERS, 4)),
+            pltpu.SemaphoreType.DMA((LAYERS, 12)),
+            pltpu.SemaphoreType.DMA((LAYERS, 12)),
+        ],
+        compiler_params=pltpu.CompilerParams(
+            collective_id=0, has_side_effects=True, vmem_limit_bytes=60 * 1024 * 1024
+        ),
+    )(
+        share,
+        row_time,
+        key_time,
+        ln1_gain[:, None],
+        ln1_bias[:, None],
+        qkv_bias[:, :, None],
+        out_bias[:, None],
+        ln2_gain[:, None],
+        ln2_bias[:, None],
+        fc1_bias[:, None],
+        fc2_bias[:, None],
+        qkv_weight,
+        out_weight,
+        fc1_weight,
+        fc2_weight,
+    )
+    new_share = new_share[:share_rows]
+    cols = jnp.stack(jnp.split(new_share, tensor_size, axis=1))
+    cols = lax.all_to_all(cols, "tensor", 0, 0, tiled=True)
+    cols = cols.reshape(piece_count, piece_rows, share_cols)
+    cols = lax.all_to_all(cols, "tm", 0, 0, tiled=True)
+    cols = cols.reshape(tensor_size, share_rows, share_cols)
+    cols = lax.all_to_all(cols, "tensor", 0, 0, tiled=True)
+    return cols.transpose(1, 0, 2).reshape(1, share_rows, D)
+
+
+def shards(frames_in, frame_time, cond_count, *rest):
+    frame_split = lax.axis_size("tm") // frame_time.shape[0]
+    piece_rows = PATCH_DEV + COND // frame_split
+    seq_count = frames_in.shape[1] // piece_rows
+    by_clip = seq_count == lax.axis_size("tm") and lax.axis_size("tensor") == 4
+    body = shards_clip if by_clip else shards_gather
+    return body(frames_in, frame_time, cond_count, *rest)
+
+
 def solution(mesh):
     in_specs = (
         P("tm", None, None),

time: 457 us -> 159 us (0.35)
  waiting for transfers between devices: 151 us -> 7.39 us
  other arithmetic: 92 us -> 1.6 us
  Pallas kernels: 0 us -> 88.5 us
  matrix products: 57.9 us -> 0 us
  local copies, waits for them, and re-layouts: 69.3 us -> 18.5 us
  blocking collectives: 61.1 us -> 31 us
  between operations: 15 us -> 0.1 us
  starting transfers between devices: 5.62 us -> 10.8 us
    all_gather x7 -> x0, waiting for transfers between devices: 149 us -> none  [the longest x2 96.8 us: shards(): key_block = lax.all_gather(keys_mine, 'tm', axis=0, tiled=True)]
    pallas_call x0 -> x1, Pallas kernels: none -> 88.5 us  [shards_clip(): pl.pallas_call(layers_kernel, out_shape=jax.ShapeDtypeStruct((share_pad,...]
    reduce_sum x12 -> x0, other arithmetic: 68.3 us -> none  [the longest x2 62.4 us: shards(): total_new = jnp.sum(weights, axis=(3, 4))]
    unnamed x4 -> x0, blocking collectives: 61.1 us -> none
    dot_general x10 -> x0, matrix products: 57.9 us -> none  [the longest x2 17.4 us: shards(): jnp.dot(inner, fc2_layer, preferred_element_type=jnp.float32)]
    all_to_all x0 -> x3, blocking collectives: none -> 31 us  [the longest x2 17.1 us: shards_clip(): cols = lax.all_to_all(cols, 'tensor', 0, 0, tiled=True)]
    reshape x4 -> x7, local copies, waits for them, and re-layouts: 29.3 us -> 4.12 us  [the longest x1 0.92 us: shards_clip(): jnp.pad(row_time, pad, constant_values=1 << 29).reshape(all_rows, 1)]
    dot_general x2 -> x0, local copies, waits for them, and re-layouts: 21.4 us -> none  [shards(): jnp.einsum('sqhd,gskhd->shqgk', queries, keys_split, preferred_element_ty...]
  transfers between devices with their start and end apart: 11 -> 2, of which waited for: 7 -> 1; matrix products, arithmetic and copies ran while one was open for 31% -> 9% of each run, Pallas kernels for 0% -> 0%
where the time goes in v2:
time: 159 us; the launch traced here: 158 us
  Pallas kernels  88.5 us (56%)
  blocking collectives  31 us (19%)
  local copies, waits for them, and re-layouts  18.5 us (12%)
  starting transfers between devices  10.8 us (7%)
  waiting for transfers between devices  7.39 us (5%)
  other arithmetic  1.6 us (1%)
    pallas_call x1, Pallas kernels, shards_clip(): pl.pallas_call(layers_kernel, out_shape=jax.ShapeDtypeStruct((share_pad,...  88.5 us
    all_to_all x2, blocking collectives, shards_clip(): cols = lax.all_to_all(cols, 'tensor', 0, 0, tiled=True)  17.1 us
    all_to_all x1, blocking collectives, shards_clip(): cols = lax.all_to_all(cols, 'tm', 0, 0, tiled=True)  13.9 us
    all_to_all x1, waiting for transfers between devices, shards_clip(): cols = lax.all_to_all(cols, 'tm', 0, 0, tiled=True)  7.38 us
    all_to_all x1, starting transfers between devices, shards_clip(): cols = lax.all_to_all(cols, 'tm', 0, 0, tiled=True)  7.31 us
    all_to_all x1, starting transfers between devices, shards_clip(): cols = lax.all_to_all(cols, 'tensor', 0, 0, tiled=True)  3.45 us
  transfers between devices with their start and end apart: 2, of which 1 were waited for; matrix products, arithmetic and copies ran while one was open for 9% of the time, Pallas kernels for 0%

profile of v2, /device:TPU:0, one launch (start us, length us, event | category | flops | bytes accessed | tf_op | source)
XLA Modules:
  0.0 157.8 jit_solution(18363516850397444572)
XLA Ops:
  0.0 1.2 copy-done
  1.3 0.8 reshape.49
  2.1 7.3 %all-to-all-start = ((bf16[8,66,256]{2,1,0:T(8,128)(2,1)}), bf16[8,66,256]{2,1,0:T(8,128)(2,1)S(1)}, u32[]{:S(2)}, u32[]{:S(2)}) async-start(bf16[8,66,256]{2,1,0:T(8,128)(2,1)} %reshape.49), calls=%async_computation | async-start | bytes 589824 | tf_op jit(solution)/shard_map/all_to_all | solution.py:363
  9.4 0.1 or.14
  9.5 0.1 sub.9
  9.6 0.8 select_reduce_fusion
  10.4 0.8 select_reduce_fusion.1
  11.4 0.1 broadcast_in_dim.65
  11.5 0.1 lt.36
  11.6 7.4 %all-to-all-done = bf16[8,66,256]{2,1,0:T(8,128)(2,1)S(1)} async-done(((bf16[8,66,256]{2,1,0:T(8,128)(2,1)}), bf16[8,66,256]{2,1,0:T(8,128)(2,1)S(1)}, u32[]{:S(2)}, u32[]{:S(2)}) %all-to-all-start) | async-done | bytes 270368 | tf_op jit(solution)/shard_map/all_to_all | solution.py:363
  19.0 0.8 reshape.50
  19.7 3.5 %all-to-all-start.1 = ((bf16[4,132,256]{2,1,0:T(8,128)(2,1)}), bf16[4,132,256]{2,1,0:T(8,128)(2,1)S(1)}, u32[]{:S(2)}, u32[]{:S(2)}) async-start(bf16[4,132,256]{2,1,0:T(8,128)(2,1)} %reshape.50), calls=%async_computation.1 | async-start | bytes 557056 | tf_op jit(solution)/shard_map/all_to_all | solution.py:365
  23.2 0.7 reshape.53.kt_ref
  23.9 1.3 copy.27.qkvb
  25.2 1.3 broadcast_in_dim.68.g1
  26.5 1.3 broadcast_in_dim.69.b1
  27.8 1.3 broadcast_in_dim.71.ob
  29.1 1.3 broadcast_in_dim.72.g2
  30.4 1.3 broadcast_in_dim.73.b2
  31.7 1.3 broadcast_in_dim.74.f1b
  33.0 1.3 broadcast_in_dim.75.f2b
  34.3 0.9 reshape.57.qt_ref
  35.2 0.1 copy.25
  35.3 0.1 pad.18
  35.5 0.7 pad.11.share_ref
  36.2 88.5 %shard_map.145 = bf16[144,1024]{1,0:T(8,128)(2,1)} custom-call(bf16[144,1024]{1,0:T(8,128)(2,1)} %pad.11.share_ref, s32[576,1]{1,0:T(8,128)} %reshape.57.qt_ref, s32[1,576]{1,0:T(1,128)} %reshape.53.kt_ref, f32[2,1,1024]{2,1,0:T(1,128)} %broadcast_in_dim.68.g1, f32[2,1,1024]{2,1,0:T(1,128)} %broadcast_in_dim.69.b1, f32[2,3,1,256]{3,2,1,0:T(1,128)} %copy.27.qkvb, ...), custom_call_target="tpu_custom_call" | custom-call | tf_op jit(solution)/shard_map/pallas_call | solution.py:372
  124.7 1.0 slice_bitcast_fusion.3
  125.7 8.5 %all_to_all.25 = bf16[4,132,256]{2,1,0:T(8,128)(2,1)S(1)} all-to-all(bf16[4,132,256]{2,1,0:T(8,128)(2,1)S(1)} %pad_maximum_fusion), channel_id=1, replica_groups=mesh['tm'=8,'tensor'=4] {'tensor'}, dimensions={0} | all-to-all | bytes 540672 | tf_op jit(solution)/shard_map/all_to_all | solution.py:419
  134.3 13.9 %all_to_all.26 = bf16[8,66,256]{2,1,0:T(8,128)(2,1)S(1)} all-to-all(bf16[8,66,256]{2,1,0:T(8,128)(2,1)S(1)} %reshape.54), channel_id=1, replica_groups=mesh['tm'=8,'tensor'=4] {'tm'}, dimensions={0} | all-to-all | bytes 540672 | tf_op jit(solution)/shard_map/all_to_all | solution.py:421
  148.3 8.5 %all_to_all.27 = bf16[4,132,256]{2,1,0:T(8,128)(2,1)S(1)} all-to-all(bf16[4,132,256]{2,1,0:T(8,128)(2,1)S(1)} %reshape.55), channel_id=1, replica_groups=mesh['tm'=8,'tensor'=4] {'tensor'}, dimensions={0} | all-to-all | bytes 540672 | tf_op jit(solution)/shard_map/all_to_all | solution.py:423
  156.8 0.1 copy.28
  157.0 0.9 reshape.56
  (17 shorter events, 0.6 us)
Async XLA Ops:
  0.0 1.2 copy-start
  2.1 16.9 %all-to-all-start = ((bf16[8,66,256]{2,1,0:T(8,128)(2,1)}), bf16[8,66,256]{2,1,0:T(8,128)(2,1)S(1)}, u32[]{:S(2)}, u32[]{:S(2)}) async-start(bf16[8,66,256]{2,1,0:T(8,128)(2,1)} %reshape.49), calls=%async_computation | async-start | bytes 589824 | tf_op jit(solution)/shard_map/all_to_all | solution.py:363
  19.7 15.4 %all-to-all-start.1 = ((bf16[4,132,256]{2,1,0:T(8,128)(2,1)}), bf16[4,132,256]{2,1,0:T(8,128)(2,1)S(1)}, u32[]{:S(2)}, u32[]{:S(2)}) async-start(bf16[4,132,256]{2,1,0:T(8,128)(2,1)} %reshape.50), calls=%async_computation.1 | async-start | bytes 557056 | tf_op jit(solution)/shard_map/all_to_all | solution.py:365
